TPU v7x, 256 devices: a whole 4x4x8 slice. The times are simulated.
256 devices in a mesh: dp: 32 (over y, x, core), mp: 8 (over z).
Axes of the slice: x: 4, y: 4, z: 8, core: 2. Of those that a mesh axis runs over, the one named last changes fastest.
Arguments:
- clean: bfloat16 [128, 256, 1536], P('dp', None, 'mp'), may hold values from -6 to 6
- noise: bfloat16 [128, 256, 1536], P('dp', None, 'mp'), may hold values from -6 to 6
- teacher_first: bfloat16 [128, 256, 1536], P('dp', None, 'mp'), may hold values from -6 to 6
- teacher_second: bfloat16 [128, 256, 1536], P('dp', None, 'mp'), may hold values from -6 to 6
- step_index: int32 [128], P('dp'), may hold values from 8 to 32
- teacher_count: int32 [128], P('dp'), may hold values from 64 to 256
- up_master: float32 [1536, 6144], P('dp', 'mp'), may hold values from -6 to 6
- down_master: float32 [1536, 6144], P('dp', 'mp'), may hold values from -6 to 6
- up_moment: float32 [1536, 6144], P('dp', 'mp'), may hold values from -1.8 to 1.8
- down_moment: float32 [1536, 6144], P('dp', 'mp'), may hold values from -1.8 to 1.8
- up_second: float32 [1536, 6144], P('dp', 'mp'), may hold values from 0.002 to 0.032
- down_second: float32 [1536, 6144], P('dp', 'mp'), may hold values from 0.002 to 0.032
Outputs:
- new_up_master: float32 [1536, 6144], P('dp', 'mp')
- new_down_master: float32 [1536, 6144], P('dp', 'mp')
- new_up_moment: float32 [1536, 6144], P('dp', 'mp')
- new_down_moment: float32 [1536, 6144], P('dp', 'mp')
- new_up_second: float32 [1536, 6144], P('dp', 'mp')
- new_down_second: float32 [1536, 6144], P('dp', 'mp')
- loss_mean: float32 [], replicated
Inputs may be any that keep to these rules, and one draw needn't show every extreme that they name: `step_index`: student step k with 2k at most the sample's teacher_count.
All inputs are finite; a program needn't handle non-finite values.
Results may differ from a plain program's by a relative error of at most 0.002.
Values may be sent and summed in bfloat16 or wider, within the bound.
No kernel may reach another device: no remote copies, remote signals or barrier semaphores. Data moves between devices by JAX's collectives and lax.ppermute only.
A program may use at most 64 MiB of HBM per device.

v0:
```python
import functools
import math
import jax
import jax.numpy as jnp
from jax import lax
from jax.sharding import Mesh
from jax.sharding import PartitionSpec as P

DP = ("dp_0", "dp_1", "dp_2")
DP_MP = ("dp_0", "dp_1", "dp_2", "mp")
adam_count = 100.0
learn_rate = 0.05
decay_rate = 0.01


def sent_together(arrays, axis, dim, along):
    both = jnp.concatenate(arrays, axis=along)
    result, at, outs = (lax.all_gather(both, axis, axis=dim, tiled=True), 0, [])
    for a in arrays:
        outs.append(lax.slice_in_dim(result, at, at + a.shape[along], axis=along))
        at += a.shape[along]
    return tuple(outs)


def sent_together_2(arrays, axis, dim, along):
    ends, at = ([], 0)
    for a in arrays[:-1]:
        at += a.shape[along]
        ends.append(at)
    both = jnp.concatenate(arrays, axis=along)
    return tuple(
        jnp.split(lax.psum_scatter(both, axis, scatter_dimension=dim, tiled=True), ends, axis=along)
    )


def by_axis(shard, axes):
    return functools.reduce(lax.psum, axes, shard)


def gelu_pair(preact):
    tanh_arg = 0.7978845608028654 * (preact + 0.044715 * preact * preact * preact)
    tanh_val = jnp.tanh(tanh_arg)
    activation = 0.5 * preact * (1.0 + tanh_val)
    slopes = 0.5 * (1.0 + tanh_val) + 0.5 * preact * (
        1.0 - tanh_val * tanh_val
    ) * 0.7978845608028654 * (1.0 + 3.0 * 0.044715 * preact * preact)
    return (activation, slopes)


def distill_target(clean, noise, teacher_first, teacher_second, step_index, teacher_count):
    steps_float = teacher_count.astype(jnp.float32)[:, None, None]
    doubled = 2.0 * step_index.astype(jnp.float32)[:, None, None]
    quarter_turn = 0.5 * math.pi
    time_now = doubled / steps_float
    time_mid = (doubled - 1.0) / steps_float
    time_end = (doubled - 2.0) / steps_float
    alpha_now = jnp.cos(quarter_turn * time_now)
    sigma_now = jnp.sin(quarter_turn * time_now)
    alpha_mid = jnp.cos(quarter_turn * time_mid)
    sigma_mid = jnp.sin(quarter_turn * time_mid)
    alpha_end = jnp.cos(quarter_turn * time_end)
    sigma_end = jnp.sin(quarter_turn * time_end)
    first_f = teacher_first.astype(jnp.float32)
    second_f = teacher_second.astype(jnp.float32)
    latent_now = alpha_now * clean.astype(jnp.float32) + sigma_now * noise.astype(jnp.float32)
    noise_now = (latent_now - alpha_now * first_f) / sigma_now
    latent_mid = alpha_mid * first_f + sigma_mid * noise_now
    noise_mid = (latent_mid - alpha_mid * second_f) / sigma_mid
    latent_end = alpha_end * second_f + sigma_end * noise_mid
    sigma_ratio = sigma_end / sigma_now
    target = (latent_end - sigma_ratio * latent_now) / (alpha_end - sigma_ratio * alpha_now)
    weighting = jnp.maximum(alpha_now * alpha_now / (sigma_now * sigma_now), 1.0)[:, 0, 0]
    return (latent_now, target, weighting)


def adam_update(master, moment, second, gradient, factor):
    clipped = gradient * factor
    moment_new = 0.9 * moment + 0.1 * clipped
    second_new = 0.999 * second + 0.001 * clipped * clipped
    first_hat = moment_new / (1.0 - 0.9**adam_count)
    second_hat = second_new / (1.0 - 0.999**adam_count)
    master_new = master - learn_rate * (
        first_hat / (jnp.sqrt(second_hat) + 1e-08) + decay_rate * master
    )
    return (master_new, moment_new, second_new)


def per_device(
    clean,
    noise,
    teacher_first,
    teacher_second,
    step_index,
    teacher_count,
    up_master,
    down_master,
    up_moment,
    down_moment,
    up_second,
    down_second,
):
    samples_dev, token_count, width_local = clean.shape
    sample_total = samples_dev * lax.axis_size(DP)
    row_count = samples_dev * token_count
    latent, target, weighting = distill_target(
        clean, noise, teacher_first, teacher_second, step_index, teacher_count
    )
    noisy_rows = latent.reshape(row_count, width_local).astype(jnp.bfloat16)
    gathered = lax.all_gather(noisy_rows, "mp", axis=1, tiled=True)
    gathered_f = gathered.astype(jnp.float32)
    normed = (
        gathered_f * lax.rsqrt(jnp.mean(gathered_f * gathered_f, axis=1, keepdims=True) + 1e-06)
    ).astype(jnp.bfloat16)
    up_full, down_full = sent_together(
        (up_master.astype(jnp.bfloat16), down_master.astype(jnp.bfloat16)), DP, 0, 1
    )
    width_full = up_full.shape[0]
    hidden_local = up_full.shape[1]
    dscale = width_full ** (-0.5)
    fscale = (hidden_local * lax.axis_size("mp")) ** (-0.5)
    preact = jnp.dot(normed, up_full, preferred_element_type=jnp.float32) * dscale
    activation, slopes = gelu_pair(preact)
    hidden = activation.astype(jnp.bfloat16)
    partial_value = (
        lax.dot_general(
            hidden, down_full, (((1,), (1,)), ((), ())), preferred_element_type=jnp.float32
        )
        * fscale
    )
    branch = lax.psum_scatter(
        partial_value.astype(jnp.bfloat16), "mp", scatter_dimension=1, tiled=True
    ).astype(jnp.float32)
    errors = latent + branch.reshape(latent.shape) - target
    weight_cube = weighting[:, None, None]
    loss_part = jnp.sum(weight_cube * errors * errors)
    dpred = (
        (2.0 * weight_cube / sample_total * errors)
        .astype(jnp.bfloat16)
        .reshape(row_count, width_local)
    )
    piece = lax.all_gather(dpred, "mp", axis=1, tiled=True)
    summed = jnp.dot(piece, down_full, preferred_element_type=jnp.float32)
    grad_piece = (
        lax.dot_general(piece, hidden, (((0,), (0,)), ((), ())), preferred_element_type=jnp.float32)
        * fscale
    )
    dpre = (summed * fscale * slopes).astype(jnp.bfloat16)
    grad_up = (
        lax.dot_general(normed, dpre, (((0,), (0,)), ((), ())), preferred_element_type=jnp.float32)
        * dscale
    )
    owned_up, owned_down = sent_together_2((grad_up, grad_piece), DP, 0, 1)
    squares = jnp.sum(owned_up * owned_up) + jnp.sum(owned_down * owned_down)
    loss_total, square_total = (by_axis(loss_part, DP_MP), by_axis(squares, DP_MP))
    clip_limit = math.sqrt(2.0 * width_full * hidden_local * lax.axis_size("mp"))
    factor = clip_limit / jnp.maximum(jnp.sqrt(square_total), clip_limit)
    new_up, up_m, up_v = adam_update(up_master, up_moment, up_second, owned_up, factor)
    new_down, down_m, down_v = adam_update(
        down_master, down_moment, down_second, owned_down, factor
    )
    loss_mean = loss_total / (sample_total * token_count * width_full)
    return (new_up, new_down, up_m, down_m, up_v, down_v, loss_mean)


def solution(mesh):
    split = Mesh(mesh.devices.reshape(4, 4, 2, mesh.shape["mp"]), ("dp_0", "dp_1", "dp_2", "mp"))
    placed = (
        P(DP, None, "mp"),
        P(DP, None, "mp"),
        P(DP, None, "mp"),
        P(DP, None, "mp"),
        P(DP),
        P(DP),
        P(DP, "mp"),
        P(DP, "mp"),
        P(DP, "mp"),
        P(DP, "mp"),
        P(DP, "mp"),
        P(DP, "mp"),
    )
    return jax.shard_map(
        per_device,
        mesh=split,
        in_specs=placed,
        out_specs=(
            P(DP, "mp"),
            P(DP, "mp"),
            P(DP, "mp"),
            P(DP, "mp"),
            P(DP, "mp"),
            P(DP, "mp"),
            P(),
        ),
        check_vma=False,
    )
```

profile of v0, /device:TPU:2, one launch (start us, length us, event | category | flops | bytes accessed | tf_op | source)
XLA Modules:
  0.0 404.3 jit_solution(1169654670336712328)
XLA Ops:
  7.2 0.7 fusion.39
  8.0 1.3 fusion.27
  9.3 0.8 copy.76
  10.2 0.9 convert_element_type.57
  11.2 0.9 convert_element_type.58
  12.1 0.7 pad_maximum_fusion.1
  12.8 0.0 reduce-scatter.5.cloned.1.call-start
  12.8 45.4 %all-gather.4.cloned.1.call-done = bf16[1024,1536]{0,1:T(8,128)(2,1)} async-done(((bf16[1024,192]{0,1:T(8,128)(2,1)}), bf16[1024,1536]{0,1:T(8,128)(2,1)}) %all-gather.4.cloned.1.call-update) | async-done | bytes 3145744 | tf_op jit(solution)/shard_map/all_gather | solution.py:109
  58.3 2.7 fusion
  61.0 50.3 %all-gather.6.cloned.1.call-done = bf16[1536,1536]{1,0:T(8,128)(2,1)} async-done(((bf16[48,1536]{1,0:T(8,128)(2,1)}), bf16[1536,1536]{1,0:T(8,128)(2,1)}) %all-gather.6.cloned.1.call-update) | async-done | bytes 4718608 | tf_op jit(solution)/shard_map/all_gather | solution.py:18
  111.3 4.6 %fusion.6 = f32[1024,768]{1,0:T(8,128)S(1)} fusion(bf16[1024,1536]{0,1:T(8,128)(2,1)S(1)} %copy-done, f32[1024]{0:T(1024)S(1)} %add_rsqrt_fusion, bf16[1536,1536]{1,0:T(8,128)(2,1)} %all-gather.6.cloned.1.call-done), kind=kOutput, calls=%fused_computation.14 | convolution fusion | flops 2420637696 | bytes 8654848 | tf_op jit(solution)/shard_map/dot_general | solution.py:121
  115.9 1.8 copy-done.14
  117.7 4.4 %multiply_convert_fusion = bf16[1024,1536]{0,1:T(8,128)(2,1)} fusion(bf16[1536,1536]{1,0:T(8,128)(2,1)S(1)} %copy-done.12, f32[1024,768]{1,0:T(8,128)S(1)} %fusion.6), kind=kOutput, calls=%fused_computation.5 | convolution fusion | flops 2426929152 | bytes 8650752 | tf_op jit(solution)/shard_map/dot_general | solution.py:125
  122.2 46.7 %reduce-scatter.5.cloned.1.call-done = bf16[1024,192]{0,1:T(8,128)(2,1)} async-done(((bf16[1024,1536]{0,1:T(8,128)(2,1)}), bf16[1024,192]{0,1:T(8,128)(2,1)}) %reduce-scatter.5.cloned.1.call-update) | async-done | bytes 393232 | tf_op jit(solution)/shard_map/reduce_scatter | solution.py:130
  169.0 1.1 reshape.70
  170.1 1.5 fusion.25
  171.6 0.1 fusion.28
  171.7 0.8 copy.77
  172.5 0.2 reduce-scatter.7.cloned.1.call-start
  172.8 44.4 %all-gather.8.cloned.1.call-done = bf16[1024,1536]{0,1:T(8,128)(2,1)} async-done(((bf16[1024,192]{0,1:T(8,128)(2,1)}), bf16[1024,1536]{0,1:T(8,128)(2,1)}) %all-gather.8.cloned.1.call-update) | async-done | bytes 3145744 | tf_op jit(solution)/shard_map/all_gather | solution.py:141
  217.2 8.1 %multiply_convert_fusion.1 = bf16[1024,768]{1,0:T(8,128)(2,1)S(1)} fusion(f32[1024,768]{1,0:T(8,128)} %copy-done.14, bf16[1024,1536]{0,1:T(8,128)(2,1)} %all-gather.8.cloned.1.call-done, bf16[1536,1536]{1,0:T(8,128)(2,1)} %all-gather.6.cloned.1.call-done), kind=kOutput, calls=%fused_computation.11 | convolution fusion | flops 2432434176 | bytes 10223616 | tf_op jit(solution)/shard_map/dot_general | solution.py:142
  225.3 5.2 %convolution_multiply_fusion = f32[1536,768]{0,1:T(8,128)S(1)} fusion(bf16[1024,1536]{0,1:T(8,128)(2,1)S(1)} %copy-done.13, f32[1024,768]{1,0:T(8,128)} %copy-done.14), kind=kOutput, calls=%fused_computation.7 | convolution fusion | flops 2424963072 | bytes 11010048 | tf_op jit(solution)/shard_map/dot_general | solution.py:144
  230.5 2.8 convolution_multiply_fusion.1
  233.3 4.5 %pad_maximum_fusion = f32[1536,1536]{0,1:T(8,128)} fusion(f32[1536,768]{0,1:T(8,128)S(1)} %convolution_multiply_fusion, f32[1536,768]{0,1:T(8,128)S(1)} %convolution_multiply_fusion.1), kind=kLoop, calls=%fused_computation | loop fusion | flops 2359296 | bytes 18874368 | tf_op jit(solution)/shard_map/concatenate | solution.py:30
  237.8 9.6 %copy.73 = f32[1536,1536]{1,0:T(8,128)} copy(f32[1536,1536]{0,1:T(8,128)} %pad_maximum_fusion) | data formatting | bytes 18874368
  247.5 101.6 %reduce-scatter.7.cloned.1.call-done = f32[48,1536]{1,0:T(8,128)} async-done(((f32[1536,1536]{1,0:T(8,128)}), f32[48,1536]{1,0:T(8,128)}) %reduce-scatter.7.cloned.1.call-update) | async-done | bytes 294928 | tf_op jit(solution)/shard_map/reduce_scatter | solution.py:32
  349.1 1.6 multiply_reduce_fusion
  352.0 9.9 %all-reduce.2 = (f32[]{:T(128)}, f32[]{:T(128)}) all-reduce(f32[]{:T(128)S(6)} %add.97, f32[]{:T(128)} %get-tuple-element.44), channel_id=1, replica_groups=mesh['dp_0'=4,'dp_1'=4,'dp_2'=2,'mp'=8] {'dp_0'}, use_global_device_ids=true, to_apply=%region_5.0 | all-reduce | flops 2 | bytes 16 | tf_op jit(solution)/shard_map/psum | solution.py:37
  361.9 10.1 %all-reduce.1 = (f32[]{:T(128)}, f32[]{:T(128)}) all-reduce(f32[]{:T(128)} %get-tuple-element.34, f32[]{:T(128)} %get-tuple-element.35), channel_id=1, replica_groups=mesh['dp_0'=4,'dp_1'=4,'dp_2'=2,'mp'=8] {'dp_1'}, use_global_device_ids=true, to_apply=%region_6.0 | all-reduce | flops 2 | bytes 16 | tf_op jit(solution)/shard_map/psum | solution.py:37
  372.0 3.1 all-reduce.3
  375.1 18.1 %all-reduce = (f32[]{:T(128)}, f32[]{:T(128)}) all-reduce(f32[]{:T(128)} %get-tuple-element.36, f32[]{:T(128)} %get-tuple-element.37), channel_id=1, replica_groups=mesh['dp_0'=4,'dp_1'=4,'dp_2'=2,'mp'=8] {'mp'}, use_global_device_ids=true, to_apply=%region_8.0 | all-reduce | flops 2 | bytes 16 | tf_op jit(solution)/shard_map/psum | solution.py:37
  394.6 2.0 multiply_subtract_fusion
  (42 shorter events, 0.4 us)
Async XLA Ops:
  7.2 51.1 %all-gather.4.cloned.1.call-start = ((), (), s32[]{:S(2)}) async-start(), calls=%async_computation.2 | async-start | bytes 3538944 | tf_op jit(solution)/shard_map/all_gather | solution.py:109
  10.2 101.2 %all-gather.6.cloned.1.call-start = ((), (), s32[]{:S(2)}) async-start(), calls=%async_computation.3 | async-start | bytes 4866048 | tf_op jit(solution)/shard_map/all_gather | solution.py:18
  12.8 156.2 %reduce-scatter.5.cloned.1.call-start = ((), (), s32[]{:S(2)}) async-start(), calls=%async_computation.4 | async-start | bytes 3538944 | tf_op jit(solution)/shard_map/reduce_scatter | solution.py:130
  58.3 53.1 %copy-start = (bf16[1024,1536]{0,1:T(8,128)(2,1)S(1)}, bf16[1024,1536]{0,1:T(8,128)(2,1)}, u32[]{:S(2)}) copy-start(bf16[1024,1536]{0,1:T(8,128)(2,1)} %all-gather.4.cloned.1.call-done) | copy-start | bytes 9437188
  111.3 6.4 %copy-start.12 = (bf16[1536,1536]{1,0:T(8,128)(2,1)S(1)}, bf16[1536,1536]{1,0:T(8,128)(2,1)}, u32[]{:S(2)}) copy-start(bf16[1536,1536]{1,0:T(8,128)(2,1)} %all-gather.6.cloned.1.call-done) | copy-start | bytes 14155780
  115.9 1.8 copy-start.14
  122.1 48.0 %copy-start.2 = (bf16[4,256,192]{1,2,0:T(8,128)(2,1)S(1)}, bf16[4,256,192]{1,2,0:T(8,128)(2,1)}, u32[]{:S(2)}) copy-start(bf16[4,256,192]{1,2,0:T(8,128)(2,1)} %param.13) | copy-start | bytes 1179652
  122.1 48.0 %copy-start.3 = (bf16[4,256,192]{1,2,0:T(8,128)(2,1)S(1)}, bf16[4,256,192]{1,2,0:T(8,128)(2,1)}, u32[]{:S(2)}) copy-start(bf16[4,256,192]{1,2,0:T(8,128)(2,1)} %param.12) | copy-start | bytes 1179652
  122.1 48.0 %copy-start.6 = (bf16[4,256,192]{1,2,0:T(8,128)(2,1)S(1)}, bf16[4,256,192]{1,2,0:T(8,128)(2,1)}, u32[]{:S(2)}) copy-start(bf16[4,256,192]{1,2,0:T(8,128)(2,1)} %param.14) | copy-start | bytes 1179652
  122.1 48.0 %copy-start.7 = (bf16[4,256,192]{1,2,0:T(8,128)(2,1)S(1)}, bf16[4,256,192]{1,2,0:T(8,128)(2,1)}, u32[]{:S(2)}) copy-start(bf16[4,256,192]{1,2,0:T(8,128)(2,1)} %param.15) | copy-start | bytes 1179652
  122.1 95.1 %all-gather.8.cloned.1.call-start = ((), (), s32[]{:S(2)}) async-start(), calls=%async_computation.5 | async-start | bytes 3538944 | tf_op jit(solution)/shard_map/all_gather | solution.py:141
  172.5 176.6 %reduce-scatter.7.cloned.1.call-start = ((), (), s32[]{:S(2)}) async-start(), calls=%async_computation.6 | async-start | bytes 9732096 | tf_op jit(solution)/shard_map/reduce_scatter | solution.py:32
  217.2 8.1 %copy-start.13 = (bf16[1024,1536]{0,1:T(8,128)(2,1)S(1)}, bf16[1024,1536]{0,1:T(8,128)(2,1)}, u32[]{:S(2)}) copy-start(bf16[1024,1536]{0,1:T(8,128)(2,1)} %all-gather.8.cloned.1.call-done) | copy-start | bytes 9437188
  225.3 5.2 %copy-start.1 = (bf16[1024,1536]{0,1:T(8,128)(2,1)S(1)}, bf16[1024,1536]{0,1:T(8,128)(2,1)}, u32[]{:S(2)}) copy-start(bf16[1024,1536]{0,1:T(8,128)(2,1)} %all-gather.4.cloned.1.call-done) | copy-start | bytes 9437188
  247.5 147.1 %copy-start.4 = (f32[48,768]{1,0:T(8,128)S(1)}, f32[48,768]{1,0:T(8,128)}, u32[]{:S(2)}) copy-start(f32[48,768]{1,0:T(8,128)} %param.19) | copy-start | bytes 442372
  247.5 147.1 %copy-start.5 = (f32[48,768]{1,0:T(8,128)S(1)}, f32[48,768]{1,0:T(8,128)}, u32[]{:S(2)}) copy-start(f32[48,768]{1,0:T(8,128)} %param.18) | copy-start | bytes 442372
  247.5 147.1 %copy-start.8 = (f32[48,768]{1,0:T(8,128)S(1)}, f32[48,768]{1,0:T(8,128)}, u32[]{:S(2)}) copy-start(f32[48,768]{1,0:T(8,128)} %param.21) | copy-start | bytes 442372
  247.5 147.1 %copy-start.9 = (f32[48,768]{1,0:T(8,128)S(1)}, f32[48,768]{1,0:T(8,128)}, u32[]{:S(2)}) copy-start(f32[48,768]{1,0:T(8,128)} %param.23) | copy-start | bytes 442372
  247.5 147.1 %copy-start.10 = (f32[48,768]{1,0:T(8,128)S(1)}, f32[48,768]{1,0:T(8,128)}, u32[]{:S(2)}) copy-start(f32[48,768]{1,0:T(8,128)} %param.22) | copy-start | bytes 442372
  247.5 147.1 %copy-start.11 = (f32[48,768]{1,0:T(8,128)S(1)}, f32[48,768]{1,0:T(8,128)}, u32[]{:S(2)}) copy-start(f32[48,768]{1,0:T(8,128)} %param.20) | copy-start | bytes 442372
Sparse Core Ops, SparseCore 0:
  10.3 47.9 all-gather.3
  61.4 49.9 all-gather.5
  122.2 46.7 reduce-scatter.4
  172.6 44.4 all-gather.7
  247.6 101.4 reduce-scatter.6
where the time goes:
time: 405 us; the launch traced here: 404 us
  waiting for transfers between devices  289 us (71%)
  blocking collectives  41.1 us (10%)
  matrix products  25 us (6%)
  other arithmetic  18.2 us (4%)
  between operations  17.8 us (4%)
  local copies, waits for them, and re-layouts  13.2 us (3%)
    reduce_scatter x1, waiting for transfers between devices, sent_together_2(): lax.psum_scatter(both, axis, scatter_dimension=dim, tiled=True)  102 us
    all_gather x1, waiting for transfers between devices, sent_together(): result, at, outs = (lax.all_gather(both, axis, axis=dim, tiled=True), 0, [])  50.3 us
    reduce_scatter x1, waiting for transfers between devices, per_device(): lax.psum_scatter(partial_value.astype(jnp.bfloat16), 'mp', scatter_dimens...  46.7 us
    all_gather x1, waiting for transfers between devices, per_device(): gathered = lax.all_gather(noisy_rows, 'mp', axis=1, tiled=True)  45.4 us
    all_gather x1, waiting for transfers between devices, per_device(): piece = lax.all_gather(dpred, 'mp', axis=1, tiled=True)  44.4 us
    psum x4, blocking collectives, by_axis(): return functools.reduce(lax.psum, axes, shard)  41.1 us
    unnamed x31, local copies, waits for them, and re-layouts  11.5 us
  transfers between devices with their start and end apart: 5, of which 5 were waited for; matrix products, arithmetic and copies ran while one was open for 1% of the time, Pallas kernels for 0%

commit v1 on v0

--- a/solution.py
+++ b/solution.py
@@ -11,6 +11,12 @@
 adam_count = 100.0
 learn_rate = 0.05
 decay_rate = 0.01
+
+
+def gather_from_all(x, axis, dim):
+    size = lax.axis_size(axis)
+    repeats = [size if d == dim else 1 for d in range(x.ndim)]
+    return lax.all_to_all(jnp.tile(x, repeats), axis, split_axis=dim, concat_axis=dim, tiled=True)
 
 
 def sent_together(arrays, axis, dim, along):
@@ -106,7 +112,7 @@
         clean, noise, teacher_first, teacher_second, step_index, teacher_count
     )
     noisy_rows = latent.reshape(row_count, width_local).astype(jnp.bfloat16)
-    gathered = lax.all_gather(noisy_rows, "mp", axis=1, tiled=True)
+    gathered = gather_from_all(noisy_rows, "mp", 1)
     gathered_f = gathered.astype(jnp.float32)
     normed = (
         gathered_f * lax.rsqrt(jnp.mean(gathered_f * gathered_f, axis=1, keepdims=True) + 1e-06)

time: 405 us -> 385 us (0.951)
  waiting for transfers between devices: 289 us -> 187 us
  blocking collectives: 41.1 us -> 123 us
    all_to_all x0 -> x1, blocking collectives: none -> 81.9 us  [gather_from_all(): lax.all_to_all(jnp.tile(x, repeats), axis, split_axis=dim, concat_axis=di...]
    all_gather x1, waiting for transfers between devices: 50.3 us -> 0.02 us  [sent_together(): result, at, outs = (lax.all_gather(both, axis, axis=dim, tiled=True), 0, [])]
    all_gather x1 -> x0, waiting for transfers between devices: 45.4 us -> none  [per_device(): gathered = lax.all_gather(noisy_rows, 'mp', axis=1, tiled=True)]
    reduce_scatter x1, waiting for transfers between devices: 46.7 us -> 41 us  [per_device(): lax.psum_scatter(partial_value.astype(jnp.bfloat16), 'mp', scatter_dimens...]
    unnamed x31 -> x27, local copies, waits for them, and re-layouts: 11.5 us -> 11.3 us
  transfers between devices with their start and end apart: 5 -> 4, of which waited for: 5 -> 3; matrix products, arithmetic and copies ran while one was open for 1% -> 2% of each run, Pallas kernels for 0% -> 0%
where the time goes in v1:
time: 385 us
  waiting for transfers between devices  187 us (49%)
  blocking collectives  123 us (32%)
  matrix products  22.9 us (6%)
  other arithmetic  19.3 us (5%)
  between operations  17.8 us (5%)
  local copies, waits for them, and re-layouts  14.6 us (4%)
    reduce_scatter x1, waiting for transfers between devices, sent_together_2(): lax.psum_scatter(both, axis, scatter_dimension=dim, tiled=True)  102 us
    all_to_all x1, blocking collectives, gather_from_all(): lax.all_to_all(jnp.tile(x, repeats), axis, split_axis=dim, concat_axis=di...  81.9 us
    all_gather x1, waiting for transfers between devices, per_device(): piece = lax.all_gather(dpred, 'mp', axis=1, tiled=True)  44.4 us
    psum x4, blocking collectives, by_axis(): return functools.reduce(lax.psum, axes, shard)  41.1 us
    reduce_scatter x1, waiting for transfers between devices, per_device(): lax.psum_scatter(partial_value.astype(jnp.bfloat16), 'mp', scatter_dimens...  41 us
    unnamed x27, local copies, waits for them, and re-layouts  11.3 us
    dot_general x1, matrix products, per_device(): summed = jnp.dot(piece, down_full, preferred_element_type=jnp.float32)  7.96 us
  transfers between devices with their start and end apart: 4, of which 3 were waited for; matrix products, arithmetic and copies ran while one was open for 2% of the time, Pallas kernels for 0%

profile of v1, /device:TPU:2, one launch (start us, length us, event | category | flops | bytes accessed | tf_op | source)
XLA Modules:
  0.0 384.9 jit_solution(5067227110878487639)
XLA Ops:
  7.2 0.9 convert_element_type.69
  8.1 0.9 convert_element_type.70
  9.1 0.7 pad_maximum_fusion.1
  9.8 1.2 fusion.36
  11.1 1.3 fusion.24
  12.4 0.4 tile.2
  12.8 81.9 %all_to_all.6 = bf16[1024,8,192]{0,2,1:T(8,128)(2,1)S(1)} all-to-all(bf16[1024,8,192]{0,2,1:T(8,128)(2,1)S(1)} %tile.2), channel_id=1, replica_groups=mesh['dp_0'=4,'dp_1'=4,'dp_2'=2,'mp'=8] {'mp'}, dimensions={1} | all-to-all | bytes 6291456 | tf_op jit(solution)/shard_map/all_to_all | solution.py:19
  94.8 0.7 multiply_reduce_fusion
  95.5 0.9 fusion
  96.4 4.6 %fusion.4 = f32[1024,768]{1,0:T(8,128)S(1)} fusion(bf16[1024,1536]{0,1:T(8,128)(2,1)S(1)} %fusion, bf16[1536,1536]{1,0:T(8,128)(2,1)} %all-gather.3.cloned.1.call-done), kind=kOutput, calls=%fused_computation.13 | convolution fusion | flops 2415919104 | bytes 8650752 | tf_op jit(solution)/shard_map/dot_general | solution.py:127
  101.0 1.6 copy-done.11
  102.7 4.5 %multiply_convert_fusion = bf16[1024,1536]{0,1:T(8,128)(2,1)} fusion(bf16[1536,1536]{1,0:T(8,128)(2,1)S(1)} %copy-done.9, f32[1024,768]{1,0:T(8,128)S(1)} %fusion.4), kind=kOutput, calls=%fused_computation.3 | convolution fusion | flops 2426929152 | bytes 8650752 | tf_op jit(solution)/shard_map/dot_general | solution.py:131
  107.2 0.7 cos.13
  108.0 1.2 sin.14
  109.2 0.5 multiply_subtract_fusion.2
  109.7 41.0 %reduce-scatter.5.cloned.1.call-done = bf16[1024,192]{0,1:T(8,128)(2,1)} async-done(((bf16[1024,1536]{0,1:T(8,128)(2,1)}), bf16[1024,192]{0,1:T(8,128)(2,1)}) %reduce-scatter.5.cloned.1.call-update) | async-done | bytes 393232 | tf_op jit(solution)/shard_map/reduce_scatter | solution.py:136
  150.7 1.1 reshape.84
  151.8 2.7 fusion.22
  154.7 0.8 copy.77
  155.7 44.4 %all-gather.5.cloned.1.call-done = bf16[1024,1536]{0,1:T(8,128)(2,1)} async-done(((bf16[1024,192]{0,1:T(8,128)(2,1)}), bf16[1024,1536]{0,1:T(8,128)(2,1)}) %all-gather.5.cloned.1.call-update) | async-done | bytes 3145744 | tf_op jit(solution)/shard_map/all_gather | solution.py:147
  200.1 8.0 %multiply_convert_fusion.1 = bf16[1024,768]{1,0:T(8,128)(2,1)S(1)} fusion(f32[1024,768]{1,0:T(8,128)} %copy-done.11, bf16[1024,1536]{0,1:T(8,128)(2,1)} %all-gather.5.cloned.1.call-done, bf16[1536,1536]{1,0:T(8,128)(2,1)} %all-gather.3.cloned.1.call-done), kind=kOutput, calls=%fused_computation.10 | convolution fusion | flops 2432434176 | bytes 10223616 | tf_op jit(solution)/shard_map/dot_general | solution.py:148
  208.0 2.8 convolution_multiply_fusion.1
  210.9 3.2 convolution_multiply_fusion
  214.1 4.5 %pad_maximum_fusion = f32[1536,1536]{0,1:T(8,128)} fusion(f32[1536,768]{0,1:T(8,128)S(1)} %convolution_multiply_fusion, f32[1536,768]{0,1:T(8,128)S(1)} %convolution_multiply_fusion.1), kind=kLoop, calls=%fused_computation | loop fusion | flops 2359296 | bytes 18874368 | tf_op jit(solution)/shard_map/concatenate | solution.py:36
  218.5 9.6 %copy.73 = f32[1536,1536]{1,0:T(8,128)} copy(f32[1536,1536]{0,1:T(8,128)} %pad_maximum_fusion) | data formatting | bytes 18874368
  228.2 101.6 %reduce-scatter.7.cloned.1.call-done = f32[48,1536]{1,0:T(8,128)} async-done(((f32[1536,1536]{1,0:T(8,128)}), f32[48,1536]{1,0:T(8,128)}) %reduce-scatter.7.cloned.1.call-update) | async-done | bytes 294928 | tf_op jit(solution)/shard_map/reduce_scatter | solution.py:38
  329.8 1.6 multiply_reduce_fusion.1
  332.7 9.9 %all-reduce.2 = (f32[]{:T(128)}, f32[]{:T(128)}) all-reduce(f32[]{:T(128)S(6)} %add.97, f32[]{:T(128)} %get-tuple-element.44), channel_id=1, replica_groups=mesh['dp_0'=4,'dp_1'=4,'dp_2'=2,'mp'=8] {'dp_0'}, use_global_device_ids=true, to_apply=%region_5.0 | all-reduce | flops 2 | bytes 16 | tf_op jit(solution)/shard_map/psum | solution.py:43
  342.6 10.1 %all-reduce.1 = (f32[]{:T(128)}, f32[]{:T(128)}) all-reduce(f32[]{:T(128)} %get-tuple-element.34, f32[]{:T(128)} %get-tuple-element.35), channel_id=1, replica_groups=mesh['dp_0'=4,'dp_1'=4,'dp_2'=2,'mp'=8] {'dp_1'}, use_global_device_ids=true, to_apply=%region_6.0 | all-reduce | flops 2 | bytes 16 | tf_op jit(solution)/shard_map/psum | solution.py:43
  352.7 3.1 all-reduce.3
  355.7 18.1 %all-reduce = (f32[]{:T(128)}, f32[]{:T(128)}) all-reduce(f32[]{:T(128)} %get-tuple-element.36, f32[]{:T(128)} %get-tuple-element.37), channel_id=1, replica_groups=mesh['dp_0'=4,'dp_1'=4,'dp_2'=2,'mp'=8] {'mp'}, use_global_device_ids=true, to_apply=%region_8.0 | all-reduce | flops 2 | bytes 16 | tf_op jit(solution)/shard_map/psum | solution.py:43
  375.2 2.0 multiply_subtract_fusion
  (38 shorter events, 0.7 us)
Async XLA Ops:
  7.2 89.3 %all-gather.3.cloned.1.call-start = ((), (), s32[]{:S(2)}) async-start(), calls=%async_computation.3 | async-start | bytes 4866048 | tf_op jit(solution)/shard_map/all_gather | solution.py:24
  9.8 140.9 %reduce-scatter.5.cloned.1.call-start = ((), (), s32[]{:S(2)}) async-start(), calls=%async_computation.4 | async-start | bytes 3538944 | tf_op jit(solution)/shard_map/reduce_scatter | solution.py:136
  96.4 6.2 %copy-start.9 = (bf16[1536,1536]{1,0:T(8,128)(2,1)S(1)}, bf16[1536,1536]{1,0:T(8,128)(2,1)}, u32[]{:S(2)}) copy-start(bf16[1536,1536]{1,0:T(8,128)(2,1)} %all-gather.3.cloned.1.call-done) | copy-start | bytes 14155780
  101.0 1.7 copy-start.11
  107.1 44.7 %copy-start = (bf16[4,256,192]{1,2,0:T(8,128)(2,1)S(1)}, bf16[4,256,192]{1,2,0:T(8,128)(2,1)}, u32[]{:S(2)}) copy-start(bf16[4,256,192]{1,2,0:T(8,128)(2,1)} %param.13) | copy-start | bytes 1179652
  107.2 92.9 %all-gather.5.cloned.1.call-start = ((), (), s32[]{:S(2)}) async-start(), calls=%async_computation.5 | async-start | bytes 3538944 | tf_op jit(solution)/shard_map/all_gather | solution.py:147
  107.9 1.2 copy-start.7
  150.7 3.8 copy-start.8
  155.5 174.3 %reduce-scatter.7.cloned.1.call-start = ((), (), s32[]{:S(2)}) async-start(), calls=%async_computation.6 | async-start | bytes 9732096 | tf_op jit(solution)/shard_map/reduce_scatter | solution.py:38
  208.0 2.8 copy-start.10
  208.0 2.8 copy-start.12
  228.2 147.0 %copy-start.1 = (f32[48,768]{1,0:T(8,128)S(1)}, f32[48,768]{1,0:T(8,128)}, u32[]{:S(2)}) copy-start(f32[48,768]{1,0:T(8,128)} %param.19) | copy-start | bytes 442372
  228.2 147.0 %copy-start.2 = (f32[48,768]{1,0:T(8,128)S(1)}, f32[48,768]{1,0:T(8,128)}, u32[]{:S(2)}) copy-start(f32[48,768]{1,0:T(8,128)} %param.18) | copy-start | bytes 442372
  228.2 147.0 %copy-start.3 = (f32[48,768]{1,0:T(8,128)S(1)}, f32[48,768]{1,0:T(8,128)}, u32[]{:S(2)}) copy-start(f32[48,768]{1,0:T(8,128)} %param.21) | copy-start | bytes 442372
  228.2 147.1 %copy-start.4 = (f32[48,768]{1,0:T(8,128)S(1)}, f32[48,768]{1,0:T(8,128)}, u32[]{:S(2)}) copy-start(f32[48,768]{1,0:T(8,128)} %param.23) | copy-start | bytes 442372
  228.2 147.1 %copy-start.5 = (f32[48,768]{1,0:T(8,128)S(1)}, f32[48,768]{1,0:T(8,128)}, u32[]{:S(2)}) copy-start(f32[48,768]{1,0:T(8,128)} %param.22) | copy-start | bytes 442372
  228.2 147.1 %copy-start.6 = (f32[48,768]{1,0:T(8,128)S(1)}, f32[48,768]{1,0:T(8,128)}, u32[]{:S(2)}) copy-start(f32[48,768]{1,0:T(8,128)} %param.20) | copy-start | bytes 442372
Sparse Core Ops, SparseCore 0:
  11.1 54.2 all-gather.2
  107.3 43.3 reduce-scatter.4
  155.6 44.4 all-gather.4
  228.3 101.4 reduce-scatter.6
